TPU v7x, 128 devices: a whole 4x4x4 slice. The times are simulated.
128 devices in a mesh: fsdp: 32 (over y, z_lo, x), tp: 4 (over z_hi, core).
Axes of the slice: x: 4, y: 4, z: 4 (z_hi: 2, z_lo: 2; z = z_hi * 2 + z_lo), core: 2. Of those that a mesh axis runs over, the one named last changes fastest.
Arguments:
- partials: bfloat16 [32, 2, 5120, 1024], P('fsdp', None, None, 'tp'), may hold values from -6 to 6
- token_counts: int32 [32], P('fsdp'), may hold values from 100 to 599
- owner_map: int32 [2, 4], replicated, may hold values from 0 to 3, each once within a row
- params: float32 [2, 5120, 1024], P(None, 'fsdp', 'tp'), may hold values from -0.75 to 0.75
- moment1: float32 [2, 5120, 1024], P(None, 'fsdp', 'tp'), may hold values from -0.15625 to 0.15625
- moment2: float32 [2, 5120, 1024], P(None, 'fsdp', 'tp'), may hold values from 0.0001 to 0.004
Outputs:
- new_params: float32 [2, 5120, 1024], P(None, 'fsdp', 'tp')
- new_moment1: float32 [2, 5120, 1024], P(None, 'fsdp', 'tp')
- new_moment2: float32 [2, 5120, 1024], P(None, 'fsdp', 'tp')
- rollout_delta: bfloat16 [2, 5120, 1024], P(None, None, 'tp')
Inputs may be any that keep to these rules, and one draw needn't show every extreme that they name: `owner_map`: each row is a permutation of 0 to 3.
All inputs are finite; a program needn't handle non-finite values.
Results may differ from a plain program's by a relative error of at most 0.0004.
Values may be sent and summed in bfloat16 or wider, within the bound.
A program may use at most 64 MiB of HBM per device.

v0:
```python
import jax
import jax.numpy as jnp
from jax import lax
from jax.sharding import Mesh
from jax.sharding import PartitionSpec as P

STEP = 10
FSDP = ("fsdp_0", "fsdp_1", "fsdp_2")


def sent_to_all(value, axis):
    peers = lax.axis_size(axis)
    return lax.all_to_all(
        jnp.broadcast_to(value[None], (peers, *value.shape)), axis, 0, 0, tiled=True
    )


def over_copies(value, axis):
    everything = sent_to_all(value, axis)
    return jnp.sum(everything, axis=0)


def joined_along(tiles, dim):
    tiles = jnp.moveaxis(tiles, 0, dim)
    dims = tiles.shape
    return tiles.reshape(*dims[:dim], dims[dim] * dims[dim + 1], *dims[dim + 2 :])


def collect(value, axis, dim):
    return joined_along(sent_to_all(value, axis), dim)


def all_blocks(value, axes, order):
    tiles = value[None]
    for k in order:
        tiles = lax.all_gather(tiles, axes[k], axis=0, tiled=True)
    carried = [lax.axis_size(axes[k]) for k in reversed(order)]
    tiles = tiles.reshape(*carried, *value.shape)
    turned = sorted(range(len(order)), key=lambda place: order[len(order) - 1 - place])
    return tiles.transpose(*turned, *range(len(order), tiles.ndim)).reshape(-1, *value.shape)


def whole_of(value, axes, order, dim):
    return joined_along(all_blocks(value, axes, order), dim)


def local(partials, token_counts, owner_map, params, moment1, moment2):
    weight = token_counts.astype(jnp.float32)[0]
    total = over_copies(weight, FSDP)
    counts = collect(token_counts, FSDP, 0).astype(jnp.float32)
    arrived = lax.all_to_all(partials, FSDP, split_axis=2, concat_axis=0, tiled=True)
    summed = jnp.sum(counts[:, None, None, None] * arrived.astype(jnp.float32), axis=0)
    grad = summed / total
    first = 0.9 * moment1 + 0.1 * grad
    second = 0.999 * moment2 + 0.001 * grad * grad
    bias_one = 1.0 - 0.9**STEP
    bias_two = 1.0 - 0.999**STEP
    direction = first / bias_one / (jnp.sqrt(second / bias_two) + 1e-08)
    new_params = params - 0.001 * (direction + 0.1 * params)
    delta = direction.astype(jnp.bfloat16)
    owners = lax.axis_size("tp")
    column = lax.axis_index("tp")
    served = lax.dynamic_index_in_dim(owner_map, column, 1, keepdims=False)
    select = served[:, None] == jnp.arange(owners, dtype=jnp.int32)[None, :]
    wide = collect(delta, "tp", 2)
    block = wide.shape[2] // owners
    split = wide.reshape(wide.shape[0], wide.shape[1], owners, block)
    kept = jnp.where(select[:, None, :, None], split, jnp.zeros((), jnp.bfloat16))
    rollout = whole_of(jnp.sum(kept, axis=2), FSDP, (1, 0, 2), 1)
    return (new_params, first, second, rollout)


def solution(mesh):
    split = Mesh(
        mesh.devices.reshape(4, 2, 4, mesh.shape["tp"]), ("fsdp_0", "fsdp_1", "fsdp_2", "tp")
    )
    return jax.shard_map(
        local,
        mesh=split,
        in_specs=(
            P(FSDP, None, None, "tp"),
            P(FSDP),
            P(),
            P(None, FSDP, "tp"),
            P(None, FSDP, "tp"),
            P(None, FSDP, "tp"),
        ),
        out_specs=(
            P(None, FSDP, "tp"),
            P(None, FSDP, "tp"),
            P(None, FSDP, "tp"),
            P(None, None, "tp"),
        ),
        check_vma=False,
    )
```

profile of v0, /device:TPU:0, one launch (start us, length us, event | category | flops | bytes accessed | tf_op | source)
XLA Modules:
  0.0 244.4 jit_solution(1411335727446816097)
XLA Ops:
  7.2 0.0 copy-start
  7.8 0.6 broadcast_in_dim.41
  8.5 8.8 %all-to-all-start = ((s32[32,1,1]{2,1,0:T(1,128)}), s32[32,1,1]{2,1,0:T(1,128)S(1)}, u32[]{:S(2)}, u32[]{:S(2)}) async-start(s32[32,1,1]{2,1,0:T(1,128)} %broadcast_in_dim.41), calls=%async_computation | async-start | bytes 32768 | tf_op jit(solution)/shard_map/all_to_all | solution.py:13
  17.3 8.2 %all-to-all-done = s32[32,1,1]{2,1,0:T(1,128)S(1)} async-done(((s32[32,1,1]{2,1,0:T(1,128)}), s32[32,1,1]{2,1,0:T(1,128)S(1)}, u32[]{:S(2)}, u32[]{:S(2)}) %all-to-all-start) | async-done | bytes 160 | tf_op jit(solution)/shard_map/all_to_all | solution.py:13
  25.5 0.6 broadcast_in_dim.43
  26.1 3.8 %all-to-all-start.2 = ((f32[32,1,1]{2,1,0:T(1,128)}), f32[32,1,1]{2,1,0:T(1,128)S(1)}, u32[]{:S(2)}, u32[]{:S(2)}) async-start(f32[32,1,1]{2,1,0:T(1,128)} %broadcast_in_dim.43), calls=%async_computation.2 | async-start | bytes 32768 | tf_op jit(solution)/shard_map/all_to_all | solution.py:13
  29.9 10.8 %copy.53 = bf16[1,2,5120,256]{3,1,0,2:T(2,128)(2,1)} copy(bf16[1,2,5120,256]{3,2,1,0:T(8,128)(2,1)} %param.6) | data formatting | bytes 10485760 | tf_op args[0]
  40.8 0.0 all-to-all-done.2
  40.8 8.4 %all-to-all-start.1 = ((bf16[1,2,5120,256]{3,1,0,2:T(2,128)(2,1)}), bf16[1,2,5120,256]{3,1,0,2:T(2,128)(2,1)}, u32[]{:S(2)}, u32[]{:S(2)}) async-start(bf16[1,2,5120,256]{3,1,0,2:T(2,128)(2,1)} %copy.53), calls=%async_computation.1 | async-start | bytes 10485760 | tf_op jit(solution)/shard_map/all_to_all | solution.py:51
  49.2 0.0 copy-start.4
  49.2 0.0 copy-start.5
  49.2 0.6 reduce_sum.31
  49.9 0.3 convert_reduce_fusion
  50.2 61.0 %all-to-all-done.1 = bf16[1,2,5120,256]{3,1,0,2:T(2,128)(2,1)} async-done(((bf16[1,2,5120,256]{3,1,0,2:T(2,128)(2,1)}), bf16[1,2,5120,256]{3,1,0,2:T(2,128)(2,1)}, u32[]{:S(2)}, u32[]{:S(2)}) %all-to-all-start.1) | async-done | bytes 5242912 | tf_op jit(solution)/shard_map/all_to_all | solution.py:51
  111.2 0.0 copy-start.3
  111.2 8.3 %fusion = f32[2,160,256]{2,0,1:T(2,128)S(1)} fusion(bf16[1,2,32,160,256]{4,1,3,2,0:T(2,128)(2,1)} %bitcast.12, f32[32]{0:T(128)S(1)} %convert_reduce_fusion), kind=kLoop, calls=%fused_computation.1 | loop fusion | flops 7782400 | bytes 5570688 | tf_op jit(solution)/shard_map/reduce_sum | solution.py:52
  119.4 0.0 copy-done.4
  119.5 0.0 copy-done.5
  119.5 0.9 fusion.3
  120.4 0.0 copy-start.1
  120.4 0.0 copy-start.2
  120.4 1.0 broadcast_in_dim.45
  121.4 4.9 %all-to-all-start.3 = ((bf16[4,2,160,256]{3,2,1,0:T(8,128)(2,1)}), bf16[4,2,160,256]{3,2,1,0:T(8,128)(2,1)S(1)}, u32[]{:S(2)}, u32[]{:S(2)}) async-start(bf16[4,2,160,256]{3,2,1,0:T(8,128)(2,1)} %broadcast_in_dim.45), calls=%async_computation.3 | async-start | bytes 1310720 | tf_op jit(solution)/shard_map/all_to_all | solution.py:13
  126.2 0.0 all-gather.4.cloned.1.call-start
  126.2 0.0 copy-done
  126.2 0.2 dynamic-slice_reduce_fusion
  126.4 11.5 %all-to-all-done.3 = bf16[4,2,160,256]{3,2,1,0:T(8,128)(2,1)S(1)} async-done(((bf16[4,2,160,256]{3,2,1,0:T(8,128)(2,1)}), bf16[4,2,160,256]{3,2,1,0:T(8,128)(2,1)S(1)}, u32[]{:S(2)}, u32[]{:S(2)}) %all-to-all-start.3) | async-done | bytes 655392 | tf_op jit(solution)/shard_map/all_to_all | solution.py:13
  137.9 0.1 fusion.1
  138.1 6.4 %all-gather = bf16[4,160,256]{2,1,0:T(8,128)(2,1)} all-gather(bf16[2,160,256]{2,1,0:T(8,128)(2,1)S(1)} %fusion.1), channel_id=2, replica_groups=mesh['fsdp_0'=4,'fsdp_1'=2,'fsdp_2'=4,'tp'=4] {'fsdp_1'}, dimensions={0}, use_global_device_ids=true | all-gather | bytes 491520 | tf_op jit(solution)/shard_map/all_gather | solution.py:36
  144.5 0.0 all-gather.4.cloned.1.call-update
  144.5 0.0 all-gather.6.cloned.1.call-start
  144.6 28.2 %all-gather.4.cloned.1.call-done = bf16[8,2,160,256]{3,2,1,0:T(8,128)(2,1)} async-done(((bf16[2,2,160,256]{3,2,1,0:T(8,128)(2,1)}), bf16[8,2,160,256]{3,2,1,0:T(8,128)(2,1)}) %all-gather.4.cloned.1.call-update) | async-done | bytes 1310736 | tf_op jit(solution)/shard_map/all_gather | solution.py:36
  172.8 0.0 all-gather.6.cloned.1.call-update
  172.8 0.0 copy-done.3
  172.8 0.9 multiply_subtract_fusion
  173.7 58.2 %all-gather.6.cloned.1.call-done = bf16[32,2,160,256]{3,2,1,0:T(8,128)(2,1)} async-done(((bf16[8,2,160,256]{3,2,1,0:T(8,128)(2,1)}), bf16[32,2,160,256]{3,2,1,0:T(8,128)(2,1)}) %all-gather.6.cloned.1.call-update) | async-done | bytes 5242896 | tf_op jit(solution)/shard_map/all_gather | solution.py:36
  231.9 2.9 %copy.56 = bf16[4,2,4,2,160,256]{5,4,3,2,1,0:T(8,128)(2,1)S(1)} copy(bf16[4,2,4,2,160,256]{5,4,3,1,0,2:T(8,128)(2,1)} %bitcast.24) | data formatting | bytes 10485760 | tf_op jit(solution)/shard_map/transpose | solution.py:40
  234.8 0.0 copy-done.1
  234.8 0.0 copy-done.2
  234.8 2.8 %copy.57 = bf16[2,32,160,256]{3,2,1,0:T(8,128)(2,1)} copy(bf16[2,32,160,256]{3,2,0,1:T(8,128)(2,1)S(1)} %bitcast.23) | data formatting | bytes 10485760 | tf_op jit(solution)/shard_map/transpose | solution.py:24
  (1 shorter events, 0.0 us)
Async XLA Ops:
  7.2 119.1 %copy-start = (s32[2,4]{1,0:T(2,128)S(1)}, s32[2,4]{1,0:T(2,128)}, u32[]{:S(2)}) copy-start(s32[2,4]{1,0:T(2,128)} %param.8) | copy-start | bytes 100
  8.5 17.0 %all-to-all-start = ((s32[32,1,1]{2,1,0:T(1,128)}), s32[32,1,1]{2,1,0:T(1,128)S(1)}, u32[]{:S(2)}, u32[]{:S(2)}) async-start(s32[32,1,1]{2,1,0:T(1,128)} %broadcast_in_dim.41), calls=%async_computation | async-start | bytes 32768 | tf_op jit(solution)/shard_map/all_to_all | solution.py:13
  26.1 14.7 %all-to-all-start.2 = ((f32[32,1,1]{2,1,0:T(1,128)}), f32[32,1,1]{2,1,0:T(1,128)S(1)}, u32[]{:S(2)}, u32[]{:S(2)}) async-start(f32[32,1,1]{2,1,0:T(1,128)} %broadcast_in_dim.43), calls=%async_computation.2 | async-start | bytes 32768 | tf_op jit(solution)/shard_map/all_to_all | solution.py:13
  40.8 70.4 %all-to-all-start.1 = ((bf16[1,2,5120,256]{3,1,0,2:T(2,128)(2,1)}), bf16[1,2,5120,256]{3,1,0,2:T(2,128)(2,1)}, u32[]{:S(2)}, u32[]{:S(2)}) async-start(bf16[1,2,5120,256]{3,1,0,2:T(2,128)(2,1)} %copy.53), calls=%async_computation.1 | async-start | bytes 10485760 | tf_op jit(solution)/shard_map/all_to_all | solution.py:51
  49.2 70.2 %copy-start.4 = (f32[2,160,256]{2,1,0:T(8,128)S(1)}, f32[2,160,256]{2,1,0:T(8,128)}, u32[]{:S(2)}) copy-start(f32[2,160,256]{2,1,0:T(8,128)} %param.10) | copy-start | bytes 983044
  49.2 70.2 %copy-start.5 = (f32[2,160,256]{2,1,0:T(8,128)S(1)}, f32[2,160,256]{2,1,0:T(8,128)}, u32[]{:S(2)}) copy-start(f32[2,160,256]{2,1,0:T(8,128)} %param.11) | copy-start | bytes 983044
  111.2 61.6 %copy-start.3 = (f32[2,160,256]{2,1,0:T(8,128)S(1)}, f32[2,160,256]{2,1,0:T(8,128)}, u32[]{:S(2)}) copy-start(f32[2,160,256]{2,1,0:T(8,128)} %param.9) | copy-start | bytes 983044
  120.4 114.4 %copy-start.1 = (f32[2,160,256]{2,1,0:T(8,128)}, f32[2,160,256]{2,1,0:T(8,128)S(1)}, u32[]{:S(2)}) copy-start(f32[2,160,256]{2,1,0:T(8,128)S(1)} %get-tuple-element.17) | copy-start | bytes 983044
  120.4 114.4 %copy-start.2 = (f32[2,160,256]{2,1,0:T(8,128)}, f32[2,160,256]{2,1,0:T(8,128)S(1)}, u32[]{:S(2)}) copy-start(f32[2,160,256]{2,1,0:T(8,128)S(1)} %get-tuple-element.18) | copy-start | bytes 983044
  121.4 16.6 %all-to-all-start.3 = ((bf16[4,2,160,256]{3,2,1,0:T(8,128)(2,1)}), bf16[4,2,160,256]{3,2,1,0:T(8,128)(2,1)S(1)}, u32[]{:S(2)}, u32[]{:S(2)}) async-start(bf16[4,2,160,256]{3,2,1,0:T(8,128)(2,1)} %broadcast_in_dim.45), calls=%async_computation.3 | async-start | bytes 1310720 | tf_op jit(solution)/shard_map/all_to_all | solution.py:13
  126.2 46.6 %all-gather.4.cloned.1.call-start = ((), (), s32[]{:S(2)}) async-start(), calls=%async_computation.4 | async-start | bytes 1638400 | tf_op jit(solution)/shard_map/all_gather | solution.py:36
  144.5 87.4 %all-gather.6.cloned.1.call-start = ((), (), s32[]{:S(2)}) async-start(), calls=%async_computation.5 | async-start | bytes 6553600 | tf_op jit(solution)/shard_map/all_gather | solution.py:36
Sparse Core Ops, SparseCore 0:
  144.6 28.1 all-gather.3
  174.5 57.4 all-gather.5
where the time goes:
time: 245 us; the launch traced here: 244 us
  waiting for transfers between devices  167 us (68%)
  starting transfers between devices  25.9 us (11%)
  local copies, waits for them, and re-layouts  18.9 us (8%)
  between operations  14.8 us (6%)
  other arithmetic  11.1 us (5%)
  blocking collectives  6.41 us (3%)
    all_gather x2, waiting for transfers between devices, all_blocks(): tiles = lax.all_gather(tiles, axes[k], axis=0, tiled=True)  86.4 us
    all_to_all x1, waiting for transfers between devices, local(): lax.all_to_all(partials, FSDP, split_axis=2, concat_axis=0, tiled=True)  61 us
    all_to_all x3, waiting for transfers between devices, sent_to_all(): lax.all_to_all(jnp.broadcast_to(value[None], (peers, *value.shape)), axis...  19.8 us
    all_to_all x3, starting transfers between devices, sent_to_all(): lax.all_to_all(jnp.broadcast_to(value[None], (peers, *value.shape)), axis...  17.5 us
    unnamed x13, local copies, waits for them, and re-layouts  10.9 us
    all_to_all x1, starting transfers between devices, local(): lax.all_to_all(partials, FSDP, split_axis=2, concat_axis=0, tiled=True)  8.41 us
    reduce_sum x1, other arithmetic, local(): jnp.sum(counts[:, None, None, None] * arrived.astype(jnp.float32), axis=0)  8.25 us
    all_gather x1, blocking collectives, all_blocks(): tiles = lax.all_gather(tiles, axes[k], axis=0, tiled=True)  6.41 us
  transfers between devices with their start and end apart: 6, of which 5 were waited for; matrix products, arithmetic and copies ran while one was open for 5% of the time, Pallas kernels for 0%

commit v1 on v0

v1 whole, which is shorter than its diff:
```python
import functools

import jax
import jax.numpy as jnp
from jax import lax
from jax.experimental import pallas as pl
from jax.experimental.pallas import tpu as pltpu
from jax.sharding import Mesh
from jax.sharding import PartitionSpec as P

STEP = 10
AXES = ("y", "zl", "x", "zh", "core")
FSDP = ("y", "zl", "x")
TP = ("zh", "core")
MESH = pl.DeviceIdType.MESH
F32 = jnp.float32
BF16 = jnp.bfloat16
GROUP = 32
ORDER = (2, 1, 3, 0)


def kernel(
    part, count, owners, par, mom1, mom2,
    new_par, new_mom1, new_mom2, out,
    own, got1, sent2, total, got2, got3, weight, weight1, weight2, weight3, cand0, cand1, par_v, mom1_v, mom2_v,
    local_sem, own_sem, s1, q1, s2, q2, s3, q3, ws, wq, ts, tq, as_, aq, zs, zq, cs, cq, hs, hq,
):
    at = {name: lax.axis_index(name) for name in AXES}
    z = at["zl"]
    me_tp = at["zh"] * 2 + at["core"]
    rows = got3.shape[2]
    cols = got3.shape[3]
    half = rows // 2
    first_axis = ("x", "y")
    last_axis = ("y", "x")
    pending = []
    cands = (cand0, cand1)

    def shifted(name, by, size):
        return lax.rem(at[name] + by, size)

    def send(src, dst, ssem, rsem, device):
        copy = pltpu.make_async_remote_copy(
            src_ref=src, dst_ref=dst, send_sem=ssem, recv_sem=rsem, device_id=device, device_id_type=MESH
        )
        copy.start()
        pending.append(copy)

    def arrived(dst, ssem, rsem, device):
        pltpu.make_async_remote_copy(
            src_ref=dst, dst_ref=dst, send_sem=ssem, recv_sem=rsem, device_id=device, device_id_type=MESH
        ).wait_recv()

    other_z = {"zl": 1 - z}
    other_zh = {"zh": 1 - at["zh"]}
    other_core = {"core": 1 - at["core"]}

    state = [
        pltpu.make_async_copy(par, par_v, local_sem.at[0]),
        pltpu.make_async_copy(mom1, mom1_v, local_sem.at[1]),
        pltpu.make_async_copy(mom2, mom2_v, local_sem.at[2]),
    ]
    own_copies = {}

    def block_of(l, k, to):
        c = shifted(last_axis[l], k, 4)
        a = shifted(first_axis[l], to, 4)
        return part.at[0, c, :, a] if l == 0 else part.at[1, a, :, c]

    weight[0] = jnp.full(weight.shape[1:], count[0].astype(F32), F32)
    for l in range(2):
        for k in ORDER:
            copy = pltpu.make_async_copy(block_of(l, k, 0), own.at[l, k], own_sem.at[l, k])
            copy.start()
            own_copies[l, k] = copy
    for copy in state:
        copy.start()

    barrier = pltpu.get_barrier_semaphore()
    peers = [{n: shifted(n, d, 4)} for n in ("x", "y") for d in (1, 2, 3)] + [other_z, other_zh, other_core]
    for peer in peers:
        pl.semaphore_signal(barrier, inc=1, device_id=peer, device_id_type=MESH)
    pl.semaphore_wait(barrier, len(peers))

    def to_first(l, d):
        return {first_axis[l]: shifted(first_axis[l], d, 4)}

    def to_last(l, d):
        return {last_axis[l]: shifted(last_axis[l], d, 4)}

    for k in ORDER:
        for l in range(2):
            for d in (2, 1, 3):
                send(block_of(l, k, d), got1.at[l, d - 1, k], s1.at[l, d - 1, k], q1.at[l, d - 1, k], to_first(l, d))
        if k == ORDER[0]:
            for l in range(2):
                for d in (1, 2, 3):
                    i = l * 3 + d - 1
                    send(weight.at[0], weight1.at[i], ws.at[i], wq.at[i], to_first(l, d))

    def row_loop(body):
        def step(i, carry):
            body(pl.ds(pl.multiple_of(i * GROUP, GROUP), GROUP))
            return carry

        lax.fori_loop(0, rows // GROUP, step, 0)

    def sum_first(l, k, which, dst):
        w = [weight[0, 0:1, :]] + [weight1[l * 3 + d, 0:1, :] for d in range(3)]

        def body(r):
            t = own[l, k, which, r, :].astype(F32) * w[0]
            for d in range(3):
                t = t + got1[l, d, k, which, r, :].astype(F32) * w[d + 1]
            dst[l, k, r, :] = t

        row_loop(body)

    def stage1(l, k):
        own_copies[l, k].wait()
        for d in range(3):
            arrived(got1.at[l, d, k], s1.at[l, d, k], q1.at[l, d, k], to_first(l, d + 1))
        sum_first(l, k, 1 - z, sent2)
        sum_first(l, k, z, total)
        send(sent2.at[l, k], got2.at[l, k], s2.at[l, k], q2.at[l, k], other_z)

    def stage2(l, k):
        arrived(got2.at[l, k], s2.at[l, k], q2.at[l, k], other_z)

        def body(r):
            total[l, k, r, :] = total[l, k, r, :] + got2[l, k, r, :]

        row_loop(body)
        if k:
            send(total.at[l, k], got3.at[l, k - 1], s3.at[l, k - 1], q3.at[l, k - 1], to_last(l, k))

    for i in range(6):
        arrived(weight1.at[i], ws.at[i], wq.at[i], to_first(i // 3, i % 3 + 1))
    weight[1] = weight[0] + weight1[0] + weight1[1] + weight1[2]

    units = [(l, k) for k in ORDER for l in range(2)]
    for n, (l, k) in enumerate(units):
        stage1(l, k)
        if n == 0:
            send(weight.at[1], weight2, ws.at[6], wq.at[6], other_z)
        if n >= 2:
            if n == 2:
                arrived(weight2, ws.at[6], wq.at[6], other_z)
                weight[2] = weight[1] + weight2[...]
            stage2(*units[n - 2])
            if n == 2:
                for d in (1, 2, 3):
                    send(weight.at[2], weight3.at[d - 1], ws.at[6 + d], wq.at[6 + d], to_last(0, d))
    stage2(*units[-2])
    stage2(*units[-1])

    for copy in state:
        copy.wait()
    for d in range(3):
        arrived(weight3.at[d], ws.at[7 + d], wq.at[7 + d], to_last(0, d + 1))
    inverse = 1.0 / (weight[2] + weight3[0] + weight3[1] + weight3[2])
    scale = inverse[0:1, :]
    inv_one = 1.0 / (1.0 - 0.9**STEP)
    inv_two = 1.0 / (1.0 - 0.999**STEP)

    def update(l):
        for d in (1, 0, 2):
            arrived(got3.at[l, d], s3.at[l, d], q3.at[l, d], to_last(l, d + 1))

        def body(r):
            grad = (total[l, 0, r, :] + got3[l, 0, r, :] + got3[l, 1, r, :] + got3[l, 2, r, :]) * scale
            first = 0.9 * mom1_v[l, r, :] + 0.1 * grad
            second = 0.999 * mom2_v[l, r, :] + 0.001 * grad * grad
            direction = (first * inv_one) / (jnp.sqrt(second * inv_two) + 1e-08)
            old = par_v[l, r, :]
            new_par[l, r, :] = old - 0.001 * (direction + 0.1 * old)
            new_mom1[l, r, :] = first
            new_mom2[l, r, :] = second
            cands[l][me_tp, r, :] = direction.astype(BF16)

        row_loop(body)

    tp_zh = (1 - at["zh"]) * 2 + at["core"]
    tp_core = at["zh"] * 2 + 1 - at["core"]
    tp_both = (1 - at["zh"]) * 2 + 1 - at["core"]
    for l in range(2):
        update(l)
        mine = cands[l].at[me_tp]
        send(mine, mine, ts.at[l, 0], tq.at[l, 0], other_zh)
        send(mine, mine, ts.at[l, 1], tq.at[l, 1], other_core)

    def place(l, fl, zz, ll):
        return out.at[l, ll, zz, fl] if l == 0 else out.at[l, fl, zz, ll]

    def block(l, ka, oz, kc):
        a = shifted(first_axis[l], 4 - ka, 4)
        c = shifted(last_axis[l], 4 - kc, 4)
        return place(l, a, 1 - z if oz else z, c)

    def spread_last(l, p):
        b = block(l, p % 4, p // 4, 0)
        send(b, b, cs.at[l, 0, p], cq.at[l, 0, p], to_last(l, 1))
        send(b, b, cs.at[l, 1, p], cq.at[l, 1, p], to_last(l, 3))

    def spread_z(l, d):
        b = block(l, d, 0, 0)
        send(b, b, zs.at[l, d], zq.at[l, d], other_z)

    for l in range(2):
        theirs = cands[l].at[tp_zh]
        arrived(theirs, ts.at[l, 0], tq.at[l, 0], other_zh)
        send(theirs, theirs, ts.at[l, 2], tq.at[l, 2], other_core)
    for l in range(2):
        arrived(cands[l].at[tp_core], ts.at[l, 1], tq.at[l, 1], other_core)
        arrived(cands[l].at[tp_both], ts.at[l, 2], tq.at[l, 2], other_core)
        wanted = owners[l, me_tp]
        mine = block(l, 0, 0, 0)

        def body(r):
            mine[r, :] = cands[l][wanted, r, :]

        row_loop(body)
        for d in (1, 3, 2):
            send(mine, mine, as_.at[l, d - 1], aq.at[l, d - 1], to_first(l, d))
        spread_z(l, 0)
        spread_last(l, 0)

    def from_first(l, d):
        arrived(block(l, d, 0, 0), as_.at[l, d - 1], aq.at[l, d - 1], to_first(l, d))
        spread_z(l, d)
        spread_last(l, d)

    def from_z(l, d):
        arrived(block(l, d, 1, 0), zs.at[l, d], zq.at[l, d], other_z)
        spread_last(l, 4 + d)

    def relay(l, p):
        for way, (kc, to) in enumerate(((1, 1), (3, 3))):
            b = block(l, p % 4, p // 4, kc)
            arrived(b, cs.at[l, way, p], cq.at[l, way, p], to_last(l, to))
            piece = b.at[pl.ds(way * half, half)]
            send(piece, piece, hs.at[l, way, p], hq.at[l, way, p], to_last(l, to))

    steps = [
        (from_first, 1), (from_first, 3), (relay, 0), (from_z, 0), (from_first, 2), (relay, 1), (relay, 3), (relay, 4),
        (from_z, 1), (from_z, 3), (from_z, 2), (relay, 2), (relay, 5), (relay, 7), (relay, 6),
    ]
    for step, i in steps:
        for l in range(2):
            step(l, i)
    for _, i in [s for s in steps if s[0] is relay]:
        for l in range(2):
            for way in range(2):
                b = block(l, i % 4, i // 4, 2).at[pl.ds(way * half, half)]
                arrived(b, hs.at[l, way, i], hq.at[l, way, i], to_last(l, 1 + 2 * way))
    for copy in pending:
        copy.wait_send()


def local(partials, token_counts, owner_map, params, moment1, moment2):
    layers, shard, cols = params.shape
    blocks = partials.reshape(layers, 4, 2, 4, shard, cols)
    hbm = pl.BlockSpec(memory_space=pltpu.HBM)
    smem = pl.BlockSpec(memory_space=pltpu.SMEM)
    vmem = pl.BlockSpec(memory_space=pltpu.VMEM)
    dma = pltpu.SemaphoreType.DMA
    tile = (shard, cols)
    new_params, first, second, rollout = pl.pallas_call(
        kernel,
        out_shape=(
            pltpu.VMEM(params.shape, F32),
            pltpu.VMEM(params.shape, F32),
            pltpu.VMEM(params.shape, F32),
            pltpu.VMEM((layers, 4, 2, 4, *tile), BF16),
        ),
        in_specs=[hbm, smem, smem, hbm, hbm, hbm],
        out_specs=(vmem, vmem, vmem, vmem),
        scratch_shapes=[
            pltpu.VMEM((2, 4, 2, *tile), BF16),
            pltpu.VMEM((2, 3, 4, 2, *tile), BF16),
            pltpu.VMEM((2, 4, *tile), F32),
            pltpu.VMEM((2, 4, *tile), F32),
            pltpu.VMEM((2, 4, *tile), F32),
            pltpu.VMEM((2, 3, *tile), F32),
            pltpu.VMEM((3, 8, cols), F32),
            pltpu.VMEM((6, 8, cols), F32),
            pltpu.VMEM((8, cols), F32),
            pltpu.VMEM((3, 8, cols), F32),
            pltpu.VMEM((4, *tile), BF16),
            pltpu.VMEM((4, *tile), BF16),
            pltpu.VMEM(params.shape, F32),
            pltpu.VMEM(params.shape, F32),
            pltpu.VMEM(params.shape, F32),
            dma((3,)),
            dma((2, 4)),
            dma((2, 3, 4)), dma((2, 3, 4)),
            dma((2, 4)), dma((2, 4)),
            dma((2, 3)), dma((2, 3)),
            dma((10,)), dma((10,)),
            dma((2, 3)), dma((2, 3)),
            dma((2, 3)), dma((2, 3)),
            dma((2, 4)), dma((2, 4)),
            dma((2, 2, 8)), dma((2, 2, 8)),
            dma((2, 2, 8)), dma((2, 2, 8)),
        ],
        compiler_params=pltpu.CompilerParams(
            collective_id=0, has_side_effects=True, vmem_limit_bytes=56 * 2**20
        ),
        name="reduce_update_spread",
    )(blocks, token_counts, owner_map, params, moment1, moment2)
    return new_params, first, second, rollout.reshape(layers, 32 * shard, cols)


def solution(mesh):
    split = Mesh(mesh.devices.reshape(4, 2, 4, 2, 2), AXES)
    return jax.shard_map(
        local,
        mesh=split,
        in_specs=(
            P(FSDP, None, None, TP),
            P(FSDP),
            P(),
            P(None, FSDP, TP),
            P(None, FSDP, TP),
            P(None, FSDP, TP),
        ),
        out_specs=(P(None, FSDP, TP), P(None, FSDP, TP), P(None, FSDP, TP), P(None, None, TP)),
        check_vma=False,
    )
```

time: 245 us -> 93 us (0.38)
  waiting for transfers between devices: 167 us -> 0 us
  Pallas kernels: 0 us -> 87.1 us
  starting transfers between devices: 25.9 us -> 0 us
  local copies, waits for them, and re-layouts: 18.9 us -> 4.53 us
  between operations: 14.8 us -> 1.29 us
  other arithmetic: 11.1 us -> 0 us
  blocking collectives: 6.41 us -> 0 us
    pallas_call x0 -> x1, Pallas kernels: none -> 87.1 us  [local(): pl.pallas_call(kernel, out_shape=(pltpu.VMEM(params.shape, F32), pltpu.VM...]
    all_gather x2 -> x0, waiting for transfers between devices: 86.4 us -> none  [all_blocks(): tiles = lax.all_gather(tiles, axes[k], axis=0, tiled=True)]
    all_to_all x4 -> x0, waiting for transfers between devices: 80.8 us -> none  [the longest x1 61 us: local(): lax.all_to_all(partials, FSDP, split_axis=2, concat_axis=0, tiled=True)]
    all_to_all x4 -> x0, starting transfers between devices: 25.9 us -> none  [the longest x3 17.5 us: sent_to_all(): lax.all_to_all(jnp.broadcast_to(value[None], (peers, *value.shape)), axis...]
    reduce_sum x3 -> x0, other arithmetic: 9.02 us -> none  [the longest x1 8.25 us: local(): jnp.sum(counts[:, None, None, None] * arrived.astype(jnp.float32), axis=0)]
    all_gather x1 -> x0, blocking collectives: 6.41 us -> none  [all_blocks(): tiles = lax.all_gather(tiles, axes[k], axis=0, tiled=True)]
    unnamed x13 -> x4, local copies, waits for them, and re-layouts: 10.9 us -> 4.53 us
    transpose x2 -> x0, local copies, waits for them, and re-layouts: 5.62 us -> none  [the longest x1 2.86 us: all_blocks(): tiles.transpose(*turned, *range(len(order), tiles.ndim))]
  transfers between devices with their start and end apart: 6 -> 0, of which waited for: 5 -> 0; matrix products, arithmetic and copies ran while one was open for 5% -> 0% of each run, Pallas kernels for 0% -> 0%
where the time goes in v1:
time: 93 us; the launch traced here: 92.9 us
  Pallas kernels  87.1 us (94%)
  local copies, waits for them, and re-layouts  4.53 us (5%)
  between operations  1.29 us (1%)
    pallas_call x1, Pallas kernels, local(): pl.pallas_call(kernel, out_shape=(pltpu.VMEM(params.shape, F32), pltpu.VM...  87.1 us
    unnamed x4, local copies, waits for them, and re-layouts  4.53 us

profile of v1, /device:TPU:0, one launch (start us, length us, event | category | flops | bytes accessed | tf_op | source)
XLA Modules:
  0.0 92.9 jit_solution(2499074845200586396)
XLA Ops:
  1.3 87.1 %reduce_update_spread.1 = (f32[2,160,256]{2,1,0:T(8,128)S(1)}, f32[2,160,256]{2,1,0:T(8,128)S(1)}, f32[2,160,256]{2,1,0:T(8,128)S(1)}, bf16[2,4,2,4,160,256]{5,4,3,2,1,0:T(8,128)(2,1)S(1)}) custom-call(bf16[2,4,2,4,160,256]{5,4,3,2,1,0:T(8,128)(2,1)} %bitcast.3, s32[1]{0:T(128)S(6)} %copy.18.count, s32[2,4]{1,0:T(2,128)} %owners.1, f32[2,160,256]{2,1,0:T(8,128)} %par.1, ...), custom_call_target="tpu_custom_call" | custom-call | tf_op jit(solution)/shard_map/reduce_update_spread/pallas_call | solution.py:268
  88.4 0.7 copy.14
  89.1 0.7 copy.15
  89.8 0.7 copy.16
  90.5 2.4 %copy.17 = bf16[2,5120,256]{2,1,0:T(8,128)(2,1)} copy(bf16[2,5120,256]{2,1,0:T(8,128)(2,1)S(1)} %bitcast.2) | data formatting | bytes 10485760

commit v2 on v1

v2 whole, which is shorter than its diff:
```python
import jax
import jax.numpy as jnp
from jax import lax
from jax.experimental import pallas as pl
from jax.experimental.pallas import tpu as pltpu
from jax.sharding import Mesh
from jax.sharding import PartitionSpec as P

STEP = 10
AXES = ("y", "zl", "x", "zh", "core")
FSDP = ("y", "zl", "x")
TP = ("zh", "core")
MESH = pl.DeviceIdType.MESH
F32 = jnp.float32
BF16 = jnp.bfloat16
GROUP = 32
ORDER = (2, 1, 3, 0)
SPLITS = (96, 64)
STARTS = tuple(sum(SPLITS[:i]) for i in range(len(SPLITS)))
AHEAD = 2
EVENTS = [
    ("s1", 0, 0, 2), ("s1", 0, 1, 2), ("s1", 0, 0, 1), ("s1", 0, 1, 1), ("s2", 0, 0, 2), ("s2", 0, 1, 2),
    ("s1", 0, 0, 3), ("s1", 0, 1, 3), ("s2", 0, 0, 1), ("s2", 0, 1, 1), ("s1", 0, 0, 0), ("s1", 0, 1, 0),
    ("s2", 0, 0, 3), ("m", 0, 0, 1), ("m", 0, 0, 3), ("m", 0, 1, 1), ("m", 0, 1, 3), ("s2", 0, 1, 3),
    ("s1", 1, 0, 2), ("s1", 1, 1, 2), ("s2", 0, 0, 0), ("s1", 1, 0, 1), ("s1", 1, 1, 1), ("s2", 0, 1, 0),
    ("s2", 1, 0, 2), ("fin", 0, 0), ("fin", 0, 1), ("s2", 1, 1, 2), ("s2", 1, 0, 1), ("s1", 1, 0, 3),
    ("s1", 1, 1, 3), ("s2", 1, 1, 1), ("tz", 0, 0), ("tz", 0, 1), ("ag", 0, 0), ("s1", 1, 0, 0), ("s1", 1, 1, 0),
    ("ag", 0, 1), ("m", 1, 0, 1), ("m", 1, 0, 3), ("m", 1, 1, 1), ("m", 1, 1, 3), ("s2", 1, 0, 3), ("s2", 1, 1, 3),
    ("A", 0, 0, 1), ("A", 0, 0, 3), ("C", 0, 0, 0, 1), ("C", 0, 0, 0, 3), ("Z", 0, 0, 0), ("A", 0, 1, 1),
    ("A", 0, 1, 3), ("A", 0, 0, 2), ("C", 0, 1, 0, 1), ("C", 0, 1, 0, 3), ("s2", 1, 0, 0), ("A", 0, 1, 2),
    ("s2", 1, 1, 0), ("fin", 1, 1), ("fin", 1, 0), ("C", 0, 1, 1, 1), ("C", 0, 1, 1, 3), ("Z", 0, 1, 0),
    ("C", 0, 0, 1, 1), ("C", 0, 0, 1, 3), ("C", 0, 1, 3, 1), ("C", 0, 1, 3, 3), ("Z", 0, 0, 1), ("C", 0, 0, 3, 1),
    ("C", 0, 0, 3, 3), ("Z", 0, 0, 3), ("C", 0, 1, 2, 1), ("C", 0, 1, 2, 3), ("tz", 1, 1), ("C", 0, 0, 4, 1),
    ("C", 0, 0, 4, 3), ("Z", 0, 1, 1), ("tz", 1, 0), ("ag", 1, 1), ("C", 0, 0, 2, 1), ("C", 0, 0, 2, 3),
    ("C", 0, 1, 4, 1), ("C", 0, 1, 4, 3), ("Z", 0, 1, 3), ("ag", 1, 0), ("Z", 0, 0, 2), ("C", 0, 0, 5, 1),
    ("C", 0, 0, 5, 3), ("C", 0, 1, 5, 1), ("C", 0, 1, 5, 3), ("Z", 0, 1, 2), ("C", 0, 0, 7, 1), ("C", 0, 0, 7, 3),
    ("C", 1, 1, 0, 1), ("C", 1, 1, 0, 3), ("Z", 1, 1, 0), ("A", 1, 1, 1), ("A", 1, 1, 3), ("Z", 1, 0, 0),
    ("C", 0, 1, 7, 1), ("C", 0, 1, 7, 3), ("A", 1, 0, 1), ("A", 1, 0, 3), ("A", 1, 1, 2), ("C", 1, 0, 0, 1),
    ("C", 1, 0, 0, 3), ("A", 1, 0, 2), ("Z", 1, 1, 1), ("C", 0, 0, 6, 1), ("C", 0, 0, 6, 3), ("Z", 1, 1, 3),
    ("C", 0, 1, 6, 1), ("C", 0, 1, 6, 3), ("Z", 1, 0, 1), ("C", 1, 1, 4, 1), ("C", 1, 1, 4, 3), ("Z", 1, 0, 3),
    ("C", 1, 0, 4, 1), ("C", 1, 0, 4, 3), ("C", 1, 1, 1, 1), ("C", 1, 1, 1, 3), ("Z", 1, 1, 2), ("C", 1, 0, 1, 1),
    ("C", 1, 0, 1, 3), ("C", 1, 1, 3, 1), ("C", 1, 1, 3, 3), ("Z", 1, 0, 2), ("C", 1, 0, 3, 1), ("C", 1, 0, 3, 3),
    ("C", 1, 1, 2, 1), ("C", 1, 1, 2, 3), ("C", 1, 0, 2, 1), ("C", 1, 0, 2, 3), ("C", 1, 1, 5, 1),
    ("C", 1, 1, 5, 3), ("C", 1, 0, 5, 1), ("C", 1, 0, 5, 3), ("C", 1, 1, 7, 1), ("C", 1, 1, 7, 3),
    ("C", 1, 0, 7, 1), ("C", 1, 0, 7, 3), ("C", 1, 1, 6, 1), ("C", 1, 1, 6, 3), ("C", 1, 0, 6, 1),
    ("C", 1, 0, 6, 3),
]


def kernel(
    part, count_h, owners_h, par, mom1, mom2,
    new_par, new_mom1, new_mom2, out,
    count, owners, own, got1, sent2, total, got2, gotm, got3,
    weight, weight1, weight2, weight3, par_v, mom1_v, mom2_v,
    local_sem, own_sem, s1, q1, s2, q2, sm, qm, s3, q3, ws, wq, ts, tq, as_, aq, zs, zq, cs, cq, hs, hq,
    *cands,
):
    at = {name: lax.axis_index(name) for name in AXES}
    z = at["zl"]
    me_tp = at["zh"] * 2 + at["core"]
    first_axis = ("x", "y")
    last_axis = ("y", "x")
    pending = []
    ready = set()

    def rows_of(h):
        return pl.ds(STARTS[h], SPLITS[h])

    def half_of(h, way):
        n = SPLITS[h] // 2
        return pl.ds(STARTS[h] + (n if way == 3 else 0), n)

    def shifted(name, by, size):
        return lax.rem(at[name] + by, size)

    def to_first(l, d):
        return {first_axis[l]: shifted(first_axis[l], d, 4)}

    def to_last(l, d):
        return {last_axis[l]: shifted(last_axis[l], d, 4)}

    other_z = {"zl": 1 - z}
    other_zh = {"zh": 1 - at["zh"]}
    other_core = {"core": 1 - at["core"]}

    def remote(src, dst, sems, i, device):
        return pltpu.make_async_remote_copy(
            src_ref=src, dst_ref=dst, send_sem=sems[0].at[i], recv_sem=sems[1].at[i], device_id=device, device_id_type=MESH
        )

    def send(*args):
        copy = remote(*args)
        copy.start()
        pending.append(copy)

    def arrived(dst, sems, i, device):
        remote(dst, dst, sems, i, device).wait_recv()

    def block_of(h, l, k, to):
        c = shifted(last_axis[l], k, 4)
        a = shifted(first_axis[l], to, 4)
        return part.at[0, c, :, a, rows_of(h)] if l == 0 else part.at[1, a, :, c, rows_of(h)]

    scalars = [
        pltpu.make_async_copy(count_h, count, local_sem.at[3]),
        pltpu.make_async_copy(owners_h, owners, local_sem.at[4]),
    ]
    state = [
        pltpu.make_async_copy(par, par_v, local_sem.at[0]),
        pltpu.make_async_copy(mom1, mom1_v, local_sem.at[1]),
        pltpu.make_async_copy(mom2, mom2_v, local_sem.at[2]),
    ]
    own_copies = {}
    for copy in scalars:
        copy.start()
    for h in range(len(SPLITS)):
        for k in ORDER:
            for l in range(2):
                copy = pltpu.make_async_copy(block_of(h, l, k, 0), own.at[l, k, :, rows_of(h)], own_sem.at[h, l, k])
                copy.start()
                own_copies[h, l, k] = copy
    for copy in state:
        copy.start()
    for copy in scalars:
        copy.wait()
    weight[0] = jnp.full(weight.shape[1:], count[0].astype(F32), F32)

    barrier = pltpu.get_barrier_semaphore()
    peers = [{n: shifted(n, d, 4)} for n in ("x", "y") for d in (1, 2, 3)] + [other_z, other_zh, other_core]
    for peer in peers:
        pl.semaphore_signal(barrier, inc=1, device_id=peer, device_id_type=MESH)
    pl.semaphore_wait(barrier, len(peers))

    def send_first(h, k):
        for l in range(2):
            for d in (2, 1, 3):
                dst = got1.at[l, d - 1, k, :, rows_of(h)]
                send(block_of(h, l, k, d), dst, (s1, q1), (h, l, d - 1, k), to_first(l, d))

    for l in range(2):
        for d in (1, 2, 3):
            i = l * 3 + d - 1
            send(weight.at[0], weight1.at[i], (ws, wq), i, to_first(l, d))
    waiting = [(h, k) for h in range(len(SPLITS)) for k in ORDER]
    for h, k in waiting[:AHEAD]:
        send_first(h, k)
    del waiting[:AHEAD]

    def row_loop(start, size, body):
        step = GROUP if size % GROUP == 0 else 16 if size % 16 == 0 else 8

        def one(i, carry):
            body(pl.ds(pl.multiple_of(start + i * step, 8), step))
            return carry

        lax.fori_loop(0, size // step, one, 0)

    def sum_first(h, l, k, which, dst):
        w = [weight[0, 0:1, :]] + [weight1[l * 3 + d, 0:1, :] for d in range(3)]

        def body(r):
            t = own[l, k, which, r, :].astype(F32) * w[0]
            for d in range(3):
                t = t + got1[l, d, k, which, r, :].astype(F32) * w[d + 1]
            dst[l, k, r, :] = t

        row_loop(STARTS[h], SPLITS[h], body)

    def once(key):
        fresh = key not in ready
        ready.add(key)
        return fresh

    def on_first(h, l, k):
        if once("weight1"):
            for i in range(6):
                arrived(weight1.at[i], (ws, wq), i, to_first(i // 3, i % 3 + 1))
            weight[1] = weight[0] + weight1[0] + weight1[1] + weight1[2]
        own_copies[h, l, k].wait()
        for d in range(3):
            arrived(got1.at[l, d, k, :, rows_of(h)], (s1, q1), (h, l, d, k), to_first(l, d + 1))
        sum_first(h, l, k, 1 - z, sent2)
        if once("sent1"):
            send(weight.at[1], weight2, (ws, wq), 6, other_z)
        sum_first(h, l, k, z, total)
        send(sent2.at[l, k, rows_of(h)], got2.at[l, k, rows_of(h)], (s2, q2), (h, l, k), other_z)
        if not once((h, k)) and waiting:
            send_first(*waiting.pop(0))

    def give(h, l, k):
        if not once(("give", h, l, k)):
            r = rows_of(h)
            send(total.at[l, k, r], got3.at[l, k // 2, r], (s3, q3), (h, l, k // 2), to_last(l, k))

    def on_second(h, l, k):
        if once("weight2"):
            arrived(weight2, (ws, wq), 6, other_z)
            weight[2] = weight[1] + weight2[...]
        elif once("sent2"):
            for d in (1, 2, 3):
                send(weight.at[2], weight3.at[d - 1], (ws, wq), 6 + d, to_last(0, d))
        arrived(got2.at[l, k, rows_of(h)], (s2, q2), (h, l, k), other_z)

        def body(r):
            total[l, k, r, :] = total[l, k, r, :] + got2[l, k, r, :]

        row_loop(STARTS[h], SPLITS[h], body)
        if k == 2:
            for way in (1, 3):
                r = half_of(h, way)
                send(total.at[l, 2, r], gotm.at[l, r], (sm, qm), (h, l, way // 2), to_last(l, way))
        elif k:
            give(h, l, k)

    def on_merge(h, l, way):
        part_rows = half_of(h, way)
        arrived(gotm.at[l, part_rows], (sm, qm), (h, l, way // 2), to_last(l, way))

        def body(r):
            total[l, way, r, :] = total[l, way, r, :] + gotm[l, r, :]

        row_loop(part_rows.start, part_rows.size, body)
        give(h, l, way)

    inv_one = 1.0 / (1.0 - 0.9**STEP)
    inv_two = 1.0 / (1.0 - 0.999**STEP)

    def on_final(h, l):
        if once("weight3"):
            for copy in state:
                copy.wait()
            for d in range(3):
                arrived(weight3.at[d], (ws, wq), 7 + d, to_last(0, d + 1))
            weight[3] = 1.0 / (weight[2] + weight3[0] + weight3[1] + weight3[2])
        scale = weight[3, 0:1, :]
        for i in range(2):
            arrived(got3.at[l, i, rows_of(h)], (s3, q3), (h, l, i), to_last(l, 1 + 2 * i))

        def body(r):
            grad = (total[l, 0, r, :] + got3[l, 0, r, :] + got3[l, 1, r, :]) * scale
            first = 0.9 * mom1_v[l, r, :] + 0.1 * grad
            second = 0.999 * mom2_v[l, r, :] + 0.001 * grad * grad
            direction = (first * inv_one) / (jnp.sqrt(second * inv_two) + 1e-08)
            old = par_v[l, r, :]
            new_par[l, r, :] = old - 0.001 * (direction + 0.1 * old)
            new_mom1[l, r, :] = first
            new_mom2[l, r, :] = second
            cands[h * 2 + l][me_tp, r, :] = direction.astype(BF16)

        row_loop(STARTS[h], SPLITS[h], body)
        mine = cands[h * 2 + l].at[me_tp, rows_of(h)]
        send(mine, mine, (ts, tq), (h, l, 0), other_zh)
        send(mine, mine, (ts, tq), (h, l, 1), other_core)

    tp_zh = (1 - at["zh"]) * 2 + at["core"]
    tp_core = at["zh"] * 2 + 1 - at["core"]
    tp_both = (1 - at["zh"]) * 2 + 1 - at["core"]

    def on_column(h, l):
        theirs = cands[h * 2 + l].at[tp_zh, rows_of(h)]
        arrived(theirs, (ts, tq), (h, l, 0), other_zh)
        send(theirs, theirs, (ts, tq), (h, l, 2), other_core)

    def block(h, l, ka, oz, kc):
        a = shifted(first_axis[l], 4 - ka, 4)
        c = shifted(last_axis[l], 4 - kc, 4)
        zz = 1 - z if oz else z
        return out.at[l, c, zz, a, rows_of(h)] if l == 0 else out.at[l, a, zz, c, rows_of(h)]

    def half_block(h, l, p, kc, way):
        a = shifted(first_axis[l], 4 - p % 4, 4)
        c = shifted(last_axis[l], 4 - kc, 4)
        zz = 1 - z if p // 4 else z
        r = half_of(h, way)
        return out.at[l, c, zz, a, r] if l == 0 else out.at[l, a, zz, c, r]

    def spread_last(h, l, p):
        b = block(h, l, p % 4, p // 4, 0)
        for way in (1, 3):
            send(b, b, (cs, cq), (h, l, way // 2, p), to_last(l, way))

    def spread_z(h, l, d):
        b = block(h, l, d, 0, 0)
        send(b, b, (zs, zq), (h, l, d), other_z)

    def on_pick(h, l):
        cand = cands[h * 2 + l]
        arrived(cand.at[tp_core, rows_of(h)], (ts, tq), (h, l, 1), other_core)
        arrived(cand.at[tp_both, rows_of(h)], (ts, tq), (h, l, 2), other_core)
        wanted = owners[l, me_tp]
        y, x = at["y"], at["x"]

        def body(r):
            out[l, y, z, x, r, :] = cand[wanted, r, :]

        row_loop(STARTS[h], SPLITS[h], body)
        mine = block(h, l, 0, 0, 0)
        for d in (1, 3, 2):
            send(mine, mine, (as_, aq), (h, l, d - 1), to_first(l, d))
        spread_z(h, l, 0)
        spread_last(h, l, 0)

    def on_near(h, l, d):
        arrived(block(h, l, d, 0, 0), (as_, aq), (h, l, d - 1), to_first(l, d))
        spread_last(h, l, d)
        spread_z(h, l, d)

    def on_z(h, l, d):
        arrived(block(h, l, d, 1, 0), (zs, zq), (h, l, d), other_z)
        spread_last(h, l, 4 + d)

    def on_ring(h, l, p, way):
        arrived(block(h, l, p % 4, p // 4, way), (cs, cq), (h, l, way // 2, p), to_last(l, way))
        piece = half_block(h, l, p, way, way)
        send(piece, piece, (hs, hq), (h, l, way // 2, p), to_last(l, way))

    handlers = {
        "s1": on_first, "s2": on_second, "m": on_merge, "fin": on_final, "tz": on_column,
        "ag": on_pick, "A": on_near, "Z": on_z, "C": on_ring,
    }
    for name, *args in EVENTS:
        handlers[name](*args)
    for name, *args in EVENTS:
        if name == "C":
            h, l, p, way = args
            arrived(half_block(h, l, p, 2, way), (hs, hq), (h, l, way // 2, p), to_last(l, way))
    for copy in pending:
        copy.wait_send()


def flush(a, b, c, d, oa, ob, oc, od, sems):
    copies = [
        pltpu.make_async_copy(src, dst, sems.at[i])
        for i, (src, dst) in enumerate(((d, od), (a, oa), (b, ob), (c, oc)))
    ]
    for copy in copies:
        copy.start()
    for copy in copies:
        copy.wait()


def local(partials, token_counts, owner_map, params, moment1, moment2):
    layers, shard, cols = params.shape
    blocks = partials.reshape(layers, 4, 2, 4, shard, cols)
    hbm = pl.BlockSpec(memory_space=pltpu.HBM)
    vmem = pl.BlockSpec(memory_space=pltpu.VMEM)
    dma = pltpu.SemaphoreType.DMA
    tile = (shard, cols)
    parts = len(SPLITS)
    results = pl.pallas_call(
        kernel,
        out_shape=(
            pltpu.VMEM(params.shape, F32),
            pltpu.VMEM(params.shape, F32),
            pltpu.VMEM(params.shape, F32),
            pltpu.VMEM((layers, 4, 2, 4, *tile), BF16),
        ),
        in_specs=[hbm] * 6,
        out_specs=(vmem, vmem, vmem, vmem),
        scratch_shapes=[
            pltpu.SMEM((1,), jnp.int32),
            pltpu.SMEM((2, 4), jnp.int32),
            pltpu.VMEM((2, 4, 2, *tile), BF16),
            pltpu.VMEM((2, 3, 4, 2, *tile), BF16),
            pltpu.VMEM((2, 4, *tile), F32),
            pltpu.VMEM((2, 4, *tile), F32),
            pltpu.VMEM((2, 4, *tile), F32),
            pltpu.VMEM((2, *tile), F32),
            pltpu.VMEM((2, 2, *tile), F32),
            pltpu.VMEM((4, 8, cols), F32),
            pltpu.VMEM((6, 8, cols), F32),
            pltpu.VMEM((8, cols), F32),
            pltpu.VMEM((3, 8, cols), F32),
            pltpu.VMEM(params.shape, F32),
            pltpu.VMEM(params.shape, F32),
            pltpu.VMEM(params.shape, F32),
            dma((5,)),
            dma((parts, 2, 4)),
            dma((parts, 2, 3, 4)), dma((parts, 2, 3, 4)),
            dma((parts, 2, 4)), dma((parts, 2, 4)),
            dma((parts, 2, 2)), dma((parts, 2, 2)),
            dma((parts, 2, 2)), dma((parts, 2, 2)),
            dma((10,)), dma((10,)),
            dma((parts, 2, 3)), dma((parts, 2, 3)),
            dma((parts, 2, 3)), dma((parts, 2, 3)),
            dma((parts, 2, 4)), dma((parts, 2, 4)),
            dma((parts, 2, 2, 8)), dma((parts, 2, 2, 8)),
            dma((parts, 2, 2, 8)), dma((parts, 2, 2, 8)),
            *[pltpu.VMEM((4, *tile), BF16) for _ in range(2 * parts)],
        ],
        compiler_params=pltpu.CompilerParams(
            collective_id=0, has_side_effects=True, vmem_limit_bytes=56 * 2**20
        ),
        name="reduce_update_spread",
    )(blocks, token_counts, owner_map, params, moment1, moment2)
    new_params, first, second, rollout = pl.pallas_call(
        flush,
        out_shape=tuple(jax.ShapeDtypeStruct(r.shape, r.dtype) for r in results),
        in_specs=[vmem] * 4,
        out_specs=(pl.BlockSpec(memory_space=pl.ANY),) * 4,
        scratch_shapes=[dma((4,))],
        compiler_params=pltpu.CompilerParams(vmem_limit_bytes=2**20),
        name="flush",
    )(*results)
    return new_params, first, second, rollout.reshape(layers, 32 * shard, cols)


def solution(mesh):
    split = Mesh(mesh.devices.reshape(4, 2, 4, 2, 2), AXES)
    return jax.shard_map(
        local,
        mesh=split,
        in_specs=(
            P(FSDP, None, None, TP),
            P(FSDP),
            P(),
            P(None, FSDP, TP),
            P(None, FSDP, TP),
            P(None, FSDP, TP),
        ),
        out_specs=(P(None, FSDP, TP), P(None, FSDP, TP), P(None, FSDP, TP), P(None, None, TP)),
        check_vma=False,
    )
```

time: 93 us -> 86.4 us (0.929)
  local copies, waits for them, and re-layouts: 4.53 us -> 0 us
  Pallas kernels: 87.1 us -> 84.9 us
    pallas_call x1, Pallas kernels: 87.1 us -> 82.2 us  [local(): pl.pallas_call(kernel, out_shape=(pltpu.VMEM(params.shape, F32), pltpu.VM...]
    unnamed x4 -> x0, local copies, waits for them, and re-layouts: 4.53 us -> none
    pallas_call x0 -> x1, Pallas kernels: none -> 2.68 us  [local(): pl.pallas_call(flush, out_shape=tuple((jax.ShapeDtypeStruct(r.shape, r.dt...]
where the time goes in v2:
time: 86.4 us; the launch traced here: 86.2 us
  Pallas kernels  84.9 us (98%)
  between operations  1.29 us (1%)
    pallas_call x1, Pallas kernels, local(): pl.pallas_call(kernel, out_shape=(pltpu.VMEM(params.shape, F32), pltpu.VM...  82.2 us
    pallas_call x1, Pallas kernels, local(): pl.pallas_call(flush, out_shape=tuple((jax.ShapeDtypeStruct(r.shape, r.dt...  2.68 us

profile of v2, /device:TPU:0, one launch (start us, length us, event | category | flops | bytes accessed | tf_op | source)
XLA Modules:
  0.0 86.2 jit_solution(5853127233383390744)
XLA Ops:
  1.3 82.2 %reduce_update_spread.1 = (f32[2,160,256]{2,1,0:T(8,128)S(1)}, f32[2,160,256]{2,1,0:T(8,128)S(1)}, f32[2,160,256]{2,1,0:T(8,128)S(1)}, bf16[2,4,2,4,160,256]{5,4,3,2,1,0:T(8,128)(2,1)S(1)}) custom-call(bf16[2,4,2,4,160,256]{5,4,3,2,1,0:T(8,128)(2,1)} %bitcast.2, s32[1]{0:T(128)S(6)} %copy.10.count_h, s32[2,4]{1,0:T(2,128)} %owners_h.1, f32[2,160,256]{2,1,0:T(8,128)} %par.1, ...), custom_call_target="tpu_custom_call" | custom-call | tf_op jit(solution)/shard_map/reduce_update_spread/pallas_call | solution.py:350
  83.5 2.7 %flush.1 = (f32[2,160,256]{2,1,0:T(8,128)}, f32[2,160,256]{2,1,0:T(8,128)}, f32[2,160,256]{2,1,0:T(8,128)}, bf16[2,4,2,4,160,256]{5,4,3,2,1,0:T(8,128)(2,1)}) custom-call(f32[2,160,256]{2,1,0:T(8,128)S(1)} %get-tuple-element.12.a, f32[2,160,256]{2,1,0:T(8,128)S(1)} %get-tuple-element.13.b, f32[2,160,256]{2,1,0:T(8,128)S(1)} %get-tuple-element.14.c, ...), custom_call_target="tpu_custom_call" | custom-call | tf_op jit(solution)/shard_map/flush/pallas_call | solution.py:396

commit v3 on v2

v3 whole, which is shorter than its diff:
```python
import jax
import jax.numpy as jnp
from jax import lax
from jax.experimental import pallas as pl
from jax.experimental.pallas import tpu as pltpu
from jax.sharding import Mesh
from jax.sharding import PartitionSpec as P

STEP = 10
AXES = ("y", "zl", "x", "zh", "core")
FSDP = ("y", "zl", "x")
TP = ("zh", "core")
MESH = pl.DeviceIdType.MESH
F32 = jnp.float32
BF16 = jnp.bfloat16
GROUP = 32
ORDER = (2, 1, 3, 0)
SPLITS = (96, 64)
STARTS = tuple(sum(SPLITS[:i]) for i in range(len(SPLITS)))
AHEAD = 2
EVENTS = [
    ("s1", 0, 0, 2), ("s1", 0, 1, 2), ("s1", 0, 0, 1), ("s1", 0, 1, 1), ("s2", 0, 0, 2), ("s2", 0, 1, 2),
    ("s1", 0, 0, 3), ("s1", 0, 1, 3), ("s2", 0, 0, 1), ("s2", 0, 1, 1), ("s1", 0, 0, 0), ("s1", 0, 1, 0),
    ("s2", 0, 0, 3), ("m", 0, 0, 1), ("m", 0, 0, 3), ("m", 0, 1, 1), ("m", 0, 1, 3), ("s2", 0, 1, 3),
    ("s1", 1, 0, 2), ("s1", 1, 1, 2), ("s2", 0, 0, 0), ("s1", 1, 0, 1), ("s1", 1, 1, 1), ("s2", 0, 1, 0),
    ("s2", 1, 0, 2), ("fin", 0, 0), ("fin", 0, 1), ("s2", 1, 1, 2), ("s2", 1, 0, 1), ("s1", 1, 0, 3),
    ("s1", 1, 1, 3), ("s2", 1, 1, 1), ("tz", 0, 0), ("tz", 0, 1), ("ag", 0, 0), ("s1", 1, 0, 0), ("s1", 1, 1, 0),
    ("ag", 0, 1), ("m", 1, 0, 1), ("m", 1, 0, 3), ("m", 1, 1, 1), ("m", 1, 1, 3), ("s2", 1, 0, 3), ("s2", 1, 1, 3),
    ("A", 0, 0, 1), ("C", 0, 0, 0), ("Z", 0, 0, 0), ("A", 0, 1, 1), ("A", 0, 0, 2), ("C", 0, 1, 0),
    ("s2", 1, 0, 0), ("A", 0, 1, 2), ("s2", 1, 1, 0), ("fin", 1, 1), ("fin", 1, 0), ("C", 0, 1, 1), ("Z", 0, 1, 0),
    ("C", 0, 0, 1), ("C", 0, 1, 3), ("Z", 0, 0, 1), ("C", 0, 0, 3), ("Z", 0, 0, 3), ("C", 0, 1, 2), ("tz", 1, 1),
    ("C", 0, 0, 4), ("Z", 0, 1, 1), ("tz", 1, 0), ("ag", 1, 1), ("C", 0, 0, 2), ("C", 0, 1, 4), ("Z", 0, 1, 3),
    ("ag", 1, 0), ("Z", 0, 0, 2), ("C", 0, 0, 5), ("C", 0, 1, 5), ("Z", 0, 1, 2), ("C", 0, 0, 7), ("C", 1, 1, 0),
    ("Z", 1, 1, 0), ("A", 1, 1, 1), ("Z", 1, 0, 0), ("C", 0, 1, 7), ("A", 1, 0, 1), ("A", 1, 1, 2), ("C", 1, 0, 0),
    ("A", 1, 0, 2), ("Z", 1, 1, 1), ("C", 0, 0, 6), ("Z", 1, 1, 3), ("C", 0, 1, 6), ("Z", 1, 0, 1), ("C", 1, 1, 4),
    ("Z", 1, 0, 3), ("C", 1, 0, 4), ("C", 1, 1, 1), ("Z", 1, 1, 2), ("C", 1, 0, 1), ("C", 1, 1, 3), ("Z", 1, 0, 2),
    ("C", 1, 0, 3), ("C", 1, 1, 2), ("C", 1, 0, 2), ("C", 1, 1, 5), ("C", 1, 0, 5), ("C", 1, 1, 7), ("C", 1, 0, 7),
    ("C", 1, 1, 6), ("C", 1, 0, 6),
]


def kernel(
    part, count_h, owners_h, par, mom1, mom2,
    new_par, new_mom1, new_mom2, out,
    count, owners, own, got1, sent2, total, got2, gotm, got3,
    weight, weight1, weight2, weight3, state,
    local_sem, own_sem, sent, q1, q2, qm, q3, wq, tq, aq, zq, cq, hq,
    *cands,
):
    at = {name: lax.axis_index(name) for name in AXES}
    z = at["zl"]
    me_tp = at["zh"] * 2 + at["core"]
    first_axis = ("x", "y")
    last_axis = ("y", "x")
    ready = set()

    def rows_of(h):
        return pl.ds(STARTS[h], SPLITS[h])

    def half_of(h, way):
        n = SPLITS[h] // 2
        return pl.ds(STARTS[h] + (n if way == 3 else 0), n)

    def shifted(name, by, size):
        return lax.rem(at[name] + by, size)

    def to_first(l, d):
        return {first_axis[l]: shifted(first_axis[l], d, 4)}

    def to_last(l, d):
        return {last_axis[l]: shifted(last_axis[l], d, 4)}

    other_z = {"zl": 1 - z}
    other_zh = {"zh": 1 - at["zh"]}
    other_core = {"core": 1 - at["core"]}

    def send(src, dst, kind, sem, device):
        pltpu.make_async_remote_copy(
            src_ref=src, dst_ref=dst, send_sem=sent.at[kind], recv_sem=sem, device_id=device, device_id_type=MESH
        ).start()

    def arrived(ref, sem):
        pltpu.make_async_copy(ref, ref, sem).wait()

    def block_of(h, l, k, to):
        c = shifted(last_axis[l], k, 4)
        a = shifted(first_axis[l], to, 4)
        return part.at[0, c, :, a, rows_of(h)] if l == 0 else part.at[1, a, :, c, rows_of(h)]

    scalars = [
        pltpu.make_async_copy(count_h, count, local_sem.at[0]),
        pltpu.make_async_copy(owners_h, owners, local_sem.at[1]),
    ]
    for copy in scalars:
        copy.start()
    for h in range(len(SPLITS)):
        for k in ORDER:
            for l in range(2):
                pltpu.make_async_copy(block_of(h, l, k, 0), own.at[l, k, :, rows_of(h)], own_sem.at[h]).start()
    for i, source in enumerate((par, mom1, mom2)):
        pltpu.make_async_copy(source, state.at[i], local_sem.at[2]).start()
    for copy in scalars:
        copy.wait()
    weight[0] = jnp.full(weight.shape[1:], count[0].astype(F32), F32)

    barrier = pltpu.get_barrier_semaphore()
    peers = [{n: shifted(n, d, 4)} for n in ("x", "y") for d in (1, 2, 3)] + [other_z, other_zh, other_core]
    for peer in peers:
        pl.semaphore_signal(barrier, inc=1, device_id=peer, device_id_type=MESH)
    pl.semaphore_wait(barrier, len(peers))

    def send_first(h, k):
        for l in range(2):
            for d in (2, 1, 3):
                dst = got1.at[l, d - 1, k, :, rows_of(h)]
                send(block_of(h, l, k, d), dst, 0, q1.at[h, l, k], to_first(l, d))

    for l in range(2):
        for d in (1, 2, 3):
            i = l * 3 + d - 1
            send(weight.at[0], weight1.at[i], 4, wq.at[0], to_first(l, d))
    waiting = [(h, k) for h in range(len(SPLITS)) for k in ORDER]
    for h, k in waiting[:AHEAD]:
        send_first(h, k)
    del waiting[:AHEAD]

    def row_loop(start, size, body):
        step = GROUP if size % GROUP == 0 else 16 if size % 16 == 0 else 8

        def one(i, carry):
            body(pl.ds(pl.multiple_of(start + i * step, 8), step))
            return carry

        lax.fori_loop(0, size // step, one, 0)

    def sum_first(h, l, k, which, dst):
        w = [weight[0, 0:1, :]] + [weight1[l * 3 + d, 0:1, :] for d in range(3)]

        def body(r):
            t = own[l, k, which, r, :].astype(F32) * w[0]
            for d in range(3):
                t = t + got1[l, d, k, which, r, :].astype(F32) * w[d + 1]
            dst[l, k, r, :] = t

        row_loop(STARTS[h], SPLITS[h], body)

    def once(key):
        fresh = key not in ready
        ready.add(key)
        return fresh

    def on_first(h, l, k):
        if once("weight1"):
            arrived(weight1, wq.at[0])
            weight[1] = weight[0] + weight1[0] + weight1[1] + weight1[2]
        if once(("own", h)):
            arrived(own.at[:, :, :, rows_of(h)], own_sem.at[h])
        arrived(got1.at[l, :, k, :, rows_of(h)], q1.at[h, l, k])
        sum_first(h, l, k, 1 - z, sent2)
        if once("sent1"):
            send(weight.at[1], weight2, 5, wq.at[1], other_z)
        sum_first(h, l, k, z, total)
        send(sent2.at[l, k, rows_of(h)], got2.at[l, k, rows_of(h)], 1, q2.at[h, l, k], other_z)
        if not once((h, k)) and waiting:
            send_first(*waiting.pop(0))

    def give(h, l, k):
        if not once(("give", h, l, k)):
            r = rows_of(h)
            send(total.at[l, k, r], got3.at[l, k // 2, r], 3, q3.at[h, l], to_last(l, k))

    def on_second(h, l, k):
        if once("weight2"):
            arrived(weight2, wq.at[1])
            weight[2] = weight[1] + weight2[...]
        elif once("sent2"):
            for d in (1, 2, 3):
                send(weight.at[2], weight3.at[d - 1], 6, wq.at[2], to_last(0, d))
        arrived(got2.at[l, k, rows_of(h)], q2.at[h, l, k])

        def body(r):
            total[l, k, r, :] = total[l, k, r, :] + got2[l, k, r, :]

        row_loop(STARTS[h], SPLITS[h], body)
        if k == 2:
            for way in (1, 3):
                r = half_of(h, way)
                send(total.at[l, 2, r], gotm.at[l, r], 2, qm.at[h, l, way // 2], to_last(l, way))
        elif k:
            give(h, l, k)

    def on_merge(h, l, way):
        part_rows = half_of(h, way)
        arrived(gotm.at[l, part_rows], qm.at[h, l, way // 2])

        def body(r):
            total[l, way, r, :] = total[l, way, r, :] + gotm[l, r, :]

        row_loop(part_rows.start, part_rows.size, body)
        give(h, l, way)

    inv_one = 1.0 / (1.0 - 0.9**STEP)
    inv_two = 1.0 / (1.0 - 0.999**STEP)

    def on_final(h, l):
        if once("weight3"):
            arrived(state, local_sem.at[2])
            arrived(weight3, wq.at[2])
            weight[3] = 1.0 / (weight[2] + weight3[0] + weight3[1] + weight3[2])
        scale = weight[3, 0:1, :]
        arrived(got3.at[l, :, rows_of(h)], q3.at[h, l])

        def body(r):
            grad = (total[l, 0, r, :] + got3[l, 0, r, :] + got3[l, 1, r, :]) * scale
            first = 0.9 * state[1, l, r, :] + 0.1 * grad
            second = 0.999 * state[2, l, r, :] + 0.001 * grad * grad
            direction = (first * inv_one) / (jnp.sqrt(second * inv_two) + 1e-08)
            old = state[0, l, r, :]
            new_par[l, r, :] = old - 0.001 * (direction + 0.1 * old)
            new_mom1[l, r, :] = first
            new_mom2[l, r, :] = second
            cands[h * 2 + l][me_tp, r, :] = direction.astype(BF16)

        row_loop(STARTS[h], SPLITS[h], body)
        mine = cands[h * 2 + l].at[me_tp, rows_of(h)]
        send(mine, mine, 7, tq.at[h, l, 0], other_zh)
        send(mine, mine, 7, tq.at[h, l, 1], other_core)

    tp_zh = (1 - at["zh"]) * 2 + at["core"]
    tp_core = at["zh"] * 2 + 1 - at["core"]
    tp_both = (1 - at["zh"]) * 2 + 1 - at["core"]

    def on_column(h, l):
        theirs = cands[h * 2 + l].at[tp_zh, rows_of(h)]
        arrived(theirs, tq.at[h, l, 0])
        send(theirs, theirs, 7, tq.at[h, l, 1], other_core)

    def block(h, l, ka, oz, kc):
        a = shifted(first_axis[l], 4 - ka, 4)
        c = shifted(last_axis[l], 4 - kc, 4)
        zz = 1 - z if oz else z
        return out.at[l, c, zz, a, rows_of(h)] if l == 0 else out.at[l, a, zz, c, rows_of(h)]

    def half_block(h, l, p, kc, way):
        a = shifted(first_axis[l], 4 - p % 4, 4)
        c = shifted(last_axis[l], 4 - kc, 4)
        zz = 1 - z if p // 4 else z
        r = half_of(h, way)
        return out.at[l, c, zz, a, r] if l == 0 else out.at[l, a, zz, c, r]

    def spread_last(h, l, p):
        b = block(h, l, p % 4, p // 4, 0)
        for way in (1, 3):
            send(b, b, 8, cq.at[h, l, p], to_last(l, way))

    def spread_z(h, l, d):
        b = block(h, l, d, 0, 0)
        send(b, b, 9, zq.at[h, l, d], other_z)

    def on_pick(h, l):
        cand = cands[h * 2 + l]
        arrived(cand.at[pl.ds(0, 2), rows_of(h)], tq.at[h, l, 1])
        wanted = owners[l, me_tp]
        y, x = at["y"], at["x"]

        def body(r):
            out[l, y, z, x, r, :] = cand[wanted, r, :]

        row_loop(STARTS[h], SPLITS[h], body)
        mine = block(h, l, 0, 0, 0)
        for d in (1, 3, 2):
            send(mine, mine, 7, aq.at[h, l, d // 2 if d == 2 else 0], to_first(l, d))
        spread_z(h, l, 0)
        spread_last(h, l, 0)

    def on_near(h, l, d):
        if d == 2:
            arrived(block(h, l, 2, 0, 0), aq.at[h, l, 1])
        else:
            arrived(out.at[0, pl.ds(0, 2), 0, 0, rows_of(h)], aq.at[h, l, 0])
        for i in (2,) if d == 2 else (1, 3):
            spread_last(h, l, i)
            spread_z(h, l, i)

    def on_z(h, l, d):
        arrived(block(h, l, d, 1, 0), zq.at[h, l, d])
        spread_last(h, l, 4 + d)

    def on_ring(h, l, p):
        arrived(out.at[0, pl.ds(0, 2), 0, 0, rows_of(h)], cq.at[h, l, p])
        for way in (1, 3):
            piece = half_block(h, l, p, way, way)
            send(piece, piece, 10, hq.at[0], to_last(l, way))

    handlers = {
        "s1": on_first, "s2": on_second, "m": on_merge, "fin": on_final, "tz": on_column,
        "ag": on_pick, "A": on_near, "Z": on_z, "C": on_ring,
    }
    for name, *args in EVENTS:
        handlers[name](*args)
    arrived(out.at[0, pl.ds(0, 2)], hq.at[0])
    for i, ref in enumerate((
        got1, sent2, gotm, got3, weight1, weight2, weight3,
        out.at[0, pl.ds(0, 3), 0], out.at[0], out.at[0, 0], out.at[0, pl.ds(0, 2)],
    )):
        arrived(ref, sent.at[i])


def flush(a, b, c, d, oa, ob, oc, od, sems):
    copies = [
        pltpu.make_async_copy(src, dst, sems.at[i])
        for i, (src, dst) in enumerate(((d, od), (a, oa), (b, ob), (c, oc)))
    ]
    for copy in copies:
        copy.start()
    for copy in copies:
        copy.wait()


def local(partials, token_counts, owner_map, params, moment1, moment2):
    layers, shard, cols = params.shape
    blocks = partials.reshape(layers, 4, 2, 4, shard, cols)
    hbm = pl.BlockSpec(memory_space=pltpu.HBM)
    vmem = pl.BlockSpec(memory_space=pltpu.VMEM)
    dma = pltpu.SemaphoreType.DMA
    tile = (shard, cols)
    parts = len(SPLITS)
    results = pl.pallas_call(
        kernel,
        out_shape=(
            pltpu.VMEM(params.shape, F32),
            pltpu.VMEM(params.shape, F32),
            pltpu.VMEM(params.shape, F32),
            pltpu.VMEM((layers, 4, 2, 4, *tile), BF16),
        ),
        in_specs=[hbm] * 6,
        out_specs=(vmem, vmem, vmem, vmem),
        scratch_shapes=[
            pltpu.SMEM((1,), jnp.int32),
            pltpu.SMEM((2, 4), jnp.int32),
            pltpu.VMEM((2, 4, 2, *tile), BF16),
            pltpu.VMEM((2, 3, 4, 2, *tile), BF16),
            pltpu.VMEM((2, 4, *tile), F32),
            pltpu.VMEM((2, 4, *tile), F32),
            pltpu.VMEM((2, 4, *tile), F32),
            pltpu.VMEM((2, *tile), F32),
            pltpu.VMEM((2, 2, *tile), F32),
            pltpu.VMEM((4, 8, cols), F32),
            pltpu.VMEM((6, 8, cols), F32),
            pltpu.VMEM((8, cols), F32),
            pltpu.VMEM((3, 8, cols), F32),
            pltpu.VMEM((3, *params.shape), F32),
            dma((3,)),
            dma((parts,)),
            dma((11,)),
            dma((parts, 2, 4)),
            dma((parts, 2, 4)),
            dma((parts, 2, 2)),
            dma((parts, 2)),
            dma((3,)),
            dma((parts, 2, 2)),
            dma((parts, 2, 2)),
            dma((parts, 2, 4)),
            dma((parts, 2, 8)),
            dma((1,)),
            *[pltpu.VMEM((4, *tile), BF16) for _ in range(2 * parts)],
        ],
        compiler_params=pltpu.CompilerParams(
            collective_id=0, has_side_effects=True, vmem_limit_bytes=56 * 2**20
        ),
        name="reduce_update_spread",
    )(blocks, token_counts, owner_map, params, moment1, moment2)
    new_params, first, second, rollout = pl.pallas_call(
        flush,
        out_shape=tuple(jax.ShapeDtypeStruct(r.shape, r.dtype) for r in results),
        in_specs=[vmem] * 4,
        out_specs=(pl.BlockSpec(memory_space=pl.ANY),) * 4,
        scratch_shapes=[dma((4,))],
        compiler_params=pltpu.CompilerParams(vmem_limit_bytes=2**20),
        name="flush",
    )(*results)
    return new_params, first, second, rollout.reshape(layers, 32 * shard, cols)


def solution(mesh):
    split = Mesh(mesh.devices.reshape(4, 2, 4, 2, 2), AXES)
    return jax.shard_map(
        local,
        mesh=split,
        in_specs=(
            P(FSDP, None, None, TP),
            P(FSDP),
            P(),
            P(None, FSDP, TP),
            P(None, FSDP, TP),
            P(None, FSDP, TP),
        ),
        out_specs=(P(None, FSDP, TP), P(None, FSDP, TP), P(None, FSDP, TP), P(None, None, TP)),
        check_vma=False,
    )
```

time: 86.4 us -> 82.4 us (0.954)
  Pallas kernels: 84.9 us -> 81 us
    pallas_call x1, Pallas kernels: 82.2 us -> 78.3 us  [local(): pl.pallas_call(kernel, out_shape=(pltpu.VMEM(params.shape, F32), pltpu.VM...]
where the time goes in v3:
time: 82.4 us; the launch traced here: 82.3 us
  Pallas kernels  81 us (98%)
  between operations  1.29 us (2%)
    pallas_call x1, Pallas kernels, local(): pl.pallas_call(kernel, out_shape=(pltpu.VMEM(params.shape, F32), pltpu.VM...  78.3 us
    pallas_call x1, Pallas kernels, local(): pl.pallas_call(flush, out_shape=tuple((jax.ShapeDtypeStruct(r.shape, r.dt...  2.68 us

profile of v3, /device:TPU:0, one launch (start us, length us, event | category | flops | bytes accessed | tf_op | source)
XLA Modules:
  0.0 82.3 jit_solution(7772215798699159469)
XLA Ops:
  1.3 78.3 %reduce_update_spread.1 = (f32[2,160,256]{2,1,0:T(8,128)S(1)}, f32[2,160,256]{2,1,0:T(8,128)S(1)}, f32[2,160,256]{2,1,0:T(8,128)S(1)}, bf16[2,4,2,4,160,256]{5,4,3,2,1,0:T(8,128)(2,1)S(1)}) custom-call(bf16[2,4,2,4,160,256]{5,4,3,2,1,0:T(8,128)(2,1)} %bitcast.2, s32[1]{0:T(128)S(6)} %copy.10.count_h, s32[2,4]{1,0:T(2,128)} %owners_h.1, f32[2,160,256]{2,1,0:T(8,128)} %par.1, ...), custom_call_target="tpu_custom_call" | custom-call | tf_op jit(solution)/shard_map/reduce_update_spread/pallas_call | solution.py:328
  79.6 2.7 %flush.1 = (f32[2,160,256]{2,1,0:T(8,128)}, f32[2,160,256]{2,1,0:T(8,128)}, f32[2,160,256]{2,1,0:T(8,128)}, bf16[2,4,2,4,160,256]{5,4,3,2,1,0:T(8,128)(2,1)}) custom-call(f32[2,160,256]{2,1,0:T(8,128)S(1)} %get-tuple-element.12.a, f32[2,160,256]{2,1,0:T(8,128)S(1)} %get-tuple-element.13.b, f32[2,160,256]{2,1,0:T(8,128)S(1)} %get-tuple-element.14.c, ...), custom_call_target="tpu_custom_call" | custom-call | tf_op jit(solution)/shard_map/flush/pallas_call | solution.py:373

commit v4 on v3

--- a/solution.py
+++ b/solution.py
@@ -15,27 +15,35 @@
 BF16 = jnp.bfloat16
 GROUP = 32
 ORDER = (2, 1, 3, 0)
-SPLITS = (96, 64)
+SPLITS = (64, 48, 48)
 STARTS = tuple(sum(SPLITS[:i]) for i in range(len(SPLITS)))
-AHEAD = 2
+AHEAD = 3
 EVENTS = [
     ("s1", 0, 0, 2), ("s1", 0, 1, 2), ("s1", 0, 0, 1), ("s1", 0, 1, 1), ("s2", 0, 0, 2), ("s2", 0, 1, 2),
     ("s1", 0, 0, 3), ("s1", 0, 1, 3), ("s2", 0, 0, 1), ("s2", 0, 1, 1), ("s1", 0, 0, 0), ("s1", 0, 1, 0),
-    ("s2", 0, 0, 3), ("m", 0, 0, 1), ("m", 0, 0, 3), ("m", 0, 1, 1), ("m", 0, 1, 3), ("s2", 0, 1, 3),
-    ("s1", 1, 0, 2), ("s1", 1, 1, 2), ("s2", 0, 0, 0), ("s1", 1, 0, 1), ("s1", 1, 1, 1), ("s2", 0, 1, 0),
-    ("s2", 1, 0, 2), ("fin", 0, 0), ("fin", 0, 1), ("s2", 1, 1, 2), ("s2", 1, 0, 1), ("s1", 1, 0, 3),
-    ("s1", 1, 1, 3), ("s2", 1, 1, 1), ("tz", 0, 0), ("tz", 0, 1), ("ag", 0, 0), ("s1", 1, 0, 0), ("s1", 1, 1, 0),
-    ("ag", 0, 1), ("m", 1, 0, 1), ("m", 1, 0, 3), ("m", 1, 1, 1), ("m", 1, 1, 3), ("s2", 1, 0, 3), ("s2", 1, 1, 3),
-    ("A", 0, 0, 1), ("C", 0, 0, 0), ("Z", 0, 0, 0), ("A", 0, 1, 1), ("A", 0, 0, 2), ("C", 0, 1, 0),
-    ("s2", 1, 0, 0), ("A", 0, 1, 2), ("s2", 1, 1, 0), ("fin", 1, 1), ("fin", 1, 0), ("C", 0, 1, 1), ("Z", 0, 1, 0),
-    ("C", 0, 0, 1), ("C", 0, 1, 3), ("Z", 0, 0, 1), ("C", 0, 0, 3), ("Z", 0, 0, 3), ("C", 0, 1, 2), ("tz", 1, 1),
-    ("C", 0, 0, 4), ("Z", 0, 1, 1), ("tz", 1, 0), ("ag", 1, 1), ("C", 0, 0, 2), ("C", 0, 1, 4), ("Z", 0, 1, 3),
-    ("ag", 1, 0), ("Z", 0, 0, 2), ("C", 0, 0, 5), ("C", 0, 1, 5), ("Z", 0, 1, 2), ("C", 0, 0, 7), ("C", 1, 1, 0),
-    ("Z", 1, 1, 0), ("A", 1, 1, 1), ("Z", 1, 0, 0), ("C", 0, 1, 7), ("A", 1, 0, 1), ("A", 1, 1, 2), ("C", 1, 0, 0),
-    ("A", 1, 0, 2), ("Z", 1, 1, 1), ("C", 0, 0, 6), ("Z", 1, 1, 3), ("C", 0, 1, 6), ("Z", 1, 0, 1), ("C", 1, 1, 4),
-    ("Z", 1, 0, 3), ("C", 1, 0, 4), ("C", 1, 1, 1), ("Z", 1, 1, 2), ("C", 1, 0, 1), ("C", 1, 1, 3), ("Z", 1, 0, 2),
-    ("C", 1, 0, 3), ("C", 1, 1, 2), ("C", 1, 0, 2), ("C", 1, 1, 5), ("C", 1, 0, 5), ("C", 1, 1, 7), ("C", 1, 0, 7),
-    ("C", 1, 1, 6), ("C", 1, 0, 6),
+    ("s2", 0, 0, 3), ("s1", 1, 0, 2), ("s1", 1, 1, 2), ("s2", 0, 1, 3), ("m", 0, 0, 1), ("m", 0, 0, 3),
+    ("m", 0, 1, 1), ("m", 0, 1, 3), ("s2", 0, 0, 0), ("s1", 1, 0, 1), ("s1", 1, 1, 1), ("s2", 0, 1, 0),
+    ("s2", 1, 0, 2), ("s1", 1, 0, 3), ("s1", 1, 1, 3), ("s2", 1, 1, 2), ("s2", 1, 0, 1), ("s1", 1, 0, 0),
+    ("s1", 1, 1, 0), ("s2", 1, 1, 1), ("fin", 0, 0), ("fin", 0, 1), ("s2", 1, 0, 3), ("s2", 1, 1, 3),
+    ("s1", 2, 0, 2), ("s1", 2, 1, 2), ("s2", 1, 0, 0), ("m", 1, 0, 1), ("m", 1, 0, 3), ("s2", 1, 1, 0),
+    ("s1", 2, 0, 1), ("s1", 2, 1, 1), ("m", 1, 1, 1), ("m", 1, 1, 3), ("tz", 0, 0), ("tz", 0, 1), ("s2", 2, 0, 2),
+    ("ag", 0, 0), ("ag", 0, 1), ("s1", 2, 0, 3), ("s1", 2, 1, 3), ("s2", 2, 1, 2), ("s2", 2, 0, 1),
+    ("s1", 2, 0, 0), ("s1", 2, 1, 0), ("s2", 2, 1, 1), ("Z", 0, 0, 0), ("fin", 1, 0), ("fin", 1, 1),
+    ("Z", 0, 1, 0), ("m", 2, 0, 1), ("m", 2, 0, 3), ("A", 0, 0, 1), ("C", 0, 0, 0), ("s2", 2, 0, 3),
+    ("A", 0, 1, 1), ("C", 0, 1, 0), ("A", 0, 0, 2), ("s2", 2, 1, 3), ("m", 2, 1, 1), ("m", 2, 1, 3),
+    ("C", 0, 0, 4), ("A", 0, 1, 2), ("s2", 2, 0, 0), ("C", 0, 1, 4), ("s2", 2, 1, 0), ("C", 0, 0, 1),
+    ("C", 0, 1, 1), ("C", 0, 0, 3), ("C", 0, 1, 3), ("tz", 1, 0), ("fin", 2, 0), ("Z", 0, 0, 1), ("tz", 1, 1),
+    ("C", 0, 0, 2), ("Z", 0, 0, 3), ("ag", 1, 0), ("fin", 2, 1), ("ag", 1, 1), ("Z", 0, 1, 1), ("C", 0, 1, 2),
+    ("Z", 0, 1, 3), ("Z", 0, 0, 2), ("C", 0, 0, 5), ("Z", 0, 1, 2), ("A", 1, 0, 1), ("C", 0, 0, 7), ("Z", 1, 0, 0),
+    ("C", 1, 0, 0), ("tz", 2, 0), ("C", 1, 1, 0), ("A", 1, 0, 2), ("A", 1, 1, 1), ("C", 0, 1, 5), ("Z", 1, 1, 0),
+    ("tz", 2, 1), ("ag", 2, 0), ("C", 0, 0, 6), ("A", 1, 1, 2), ("C", 0, 1, 7), ("Z", 1, 0, 1), ("ag", 2, 1),
+    ("C", 0, 1, 6), ("Z", 1, 0, 3), ("C", 1, 0, 1), ("C", 1, 0, 3), ("Z", 1, 0, 2), ("C", 1, 1, 1), ("Z", 1, 1, 1),
+    ("C", 1, 0, 4), ("C", 1, 1, 3), ("Z", 1, 1, 3), ("C", 1, 0, 2), ("Z", 2, 0, 0), ("C", 1, 1, 4), ("C", 2, 0, 0),
+    ("Z", 1, 1, 2), ("A", 2, 0, 1), ("Z", 2, 1, 0), ("C", 1, 0, 5), ("C", 1, 1, 2), ("A", 2, 0, 2), ("A", 2, 1, 1),
+    ("C", 2, 1, 0), ("C", 1, 0, 7), ("A", 2, 1, 2), ("Z", 2, 0, 1), ("C", 1, 1, 5), ("C", 1, 0, 6), ("Z", 2, 0, 3),
+    ("C", 1, 1, 7), ("Z", 2, 0, 2), ("C", 2, 0, 4), ("C", 1, 1, 6), ("Z", 2, 1, 1), ("C", 2, 1, 4), ("C", 2, 0, 1),
+    ("Z", 2, 1, 3), ("C", 2, 0, 3), ("Z", 2, 1, 2), ("C", 2, 1, 1), ("C", 2, 1, 3), ("C", 2, 0, 2), ("C", 2, 1, 2),
+    ("C", 2, 0, 5), ("C", 2, 0, 7), ("C", 2, 1, 5), ("C", 2, 0, 6), ("C", 2, 1, 7), ("C", 2, 1, 6),
 ]
 
 
@@ -91,6 +99,10 @@
         pltpu.make_async_copy(count_h, count, local_sem.at[0]),
         pltpu.make_async_copy(owners_h, owners, local_sem.at[1]),
     ]
+    barrier = pltpu.get_barrier_semaphore()
+    peers = [{n: shifted(n, d, 4)} for n in ("x", "y") for d in (1, 2, 3)] + [other_z, other_zh, other_core]
+    for peer in peers:
+        pl.semaphore_signal(barrier, inc=1, device_id=peer, device_id_type=MESH)
     for copy in scalars:
         copy.start()
     for h in range(len(SPLITS)):
@@ -103,10 +115,6 @@
         copy.wait()
     weight[0] = jnp.full(weight.shape[1:], count[0].astype(F32), F32)
 
-    barrier = pltpu.get_barrier_semaphore()
-    peers = [{n: shifted(n, d, 4)} for n in ("x", "y") for d in (1, 2, 3)] + [other_z, other_zh, other_core]
-    for peer in peers:
-        pl.semaphore_signal(barrier, inc=1, device_id=peer, device_id_type=MESH)
     pl.semaphore_wait(barrier, len(peers))
 
     def send_first(h, k):
@@ -307,10 +315,8 @@
 
 
 def flush(a, b, c, d, oa, ob, oc, od, sems):
-    copies = [
-        pltpu.make_async_copy(src, dst, sems.at[i])
-        for i, (src, dst) in enumerate(((d, od), (a, oa), (b, ob), (c, oc)))
-    ]
+    pieces = [(d.at[l, i], od.at[l, i]) for l in range(2) for i in range(4)] + [(a, oa), (b, ob), (c, oc)]
+    copies = [pltpu.make_async_copy(src, dst, sems.at[i]) for i, (src, dst) in enumerate(pieces)]
     for copy in copies:
         copy.start()
     for copy in copies:
@@ -375,7 +381,7 @@
         out_shape=tuple(jax.ShapeDtypeStruct(r.shape, r.dtype) for r in results),
         in_specs=[vmem] * 4,
         out_specs=(pl.BlockSpec(memory_space=pl.ANY),) * 4,
-        scratch_shapes=[dma((4,))],
+        scratch_shapes=[dma((11,))],
         compiler_params=pltpu.CompilerParams(vmem_limit_bytes=2**20),
         name="flush",
     )(*results)

time: 82.4 us -> 77.9 us (0.945)
  Pallas kernels: 81 us -> 76.5 us
    pallas_call x1, Pallas kernels: 78.3 us -> 73.8 us  [local(): pl.pallas_call(kernel, out_shape=(pltpu.VMEM(params.shape, F32), pltpu.VM...]
where the time goes in v4:
time: 77.9 us; the launch traced here: 77.8 us
  Pallas kernels  76.5 us (98%)
  between operations  1.29 us (2%)
    pallas_call x1, Pallas kernels, local(): pl.pallas_call(kernel, out_shape=(pltpu.VMEM(params.shape, F32), pltpu.VM...  73.8 us
    pallas_call x1, Pallas kernels, local(): pl.pallas_call(flush, out_shape=tuple((jax.ShapeDtypeStruct(r.shape, r.dt...  2.73 us

profile of v4, /device:TPU:0, one launch (start us, length us, event | category | flops | bytes accessed | tf_op | source)
XLA Modules:
  0.0 77.8 jit_solution(17637892043120632872)
XLA Ops:
  1.3 73.8 %reduce_update_spread.1 = (f32[2,160,256]{2,1,0:T(8,128)S(1)}, f32[2,160,256]{2,1,0:T(8,128)S(1)}, f32[2,160,256]{2,1,0:T(8,128)S(1)}, bf16[2,4,2,4,160,256]{5,4,3,2,1,0:T(8,128)(2,1)S(1)}) custom-call(bf16[2,4,2,4,160,256]{5,4,3,2,1,0:T(8,128)(2,1)} %bitcast.2, s32[1]{0:T(128)S(6)} %copy.10.count_h, s32[2,4]{1,0:T(2,128)} %owners_h.1, f32[2,160,256]{2,1,0:T(8,128)} %par.1, ...), custom_call_target="tpu_custom_call" | custom-call | tf_op jit(solution)/shard_map/reduce_update_spread/pallas_call | solution.py:334
  75.1 2.7 %flush.1 = (f32[2,160,256]{2,1,0:T(8,128)}, f32[2,160,256]{2,1,0:T(8,128)}, f32[2,160,256]{2,1,0:T(8,128)}, bf16[2,4,2,4,160,256]{5,4,3,2,1,0:T(8,128)(2,1)}) custom-call(f32[2,160,256]{2,1,0:T(8,128)S(1)} %get-tuple-element.12.a, f32[2,160,256]{2,1,0:T(8,128)S(1)} %get-tuple-element.13.b, f32[2,160,256]{2,1,0:T(8,128)S(1)} %get-tuple-element.14.c, ...), custom_call_target="tpu_custom_call" | custom-call | tf_op jit(solution)/shard_map/flush/pallas_call | solution.py:379
